TPU v7x, 32 devices: a 4x2x2 block of a 4x4x8 slice. The times are simulated.
32 devices in a mesh: dp: 4 (over y, z), tp: 8 (over x, core).
Axes of the slice: x: 4, y: 2, z: 2, core: 2. Of those that a mesh axis runs over, the one named last changes fastest.
The devices are a block of a 4x4x8 slice.
Arguments:
- X: bfloat16 [1024, 2560], P(('dp', 'tp')), parts along dimension 0
- dY: bfloat16 [1024, 2560], P(('dp', 'tp')), parts along dimension 0
- W1: bfloat16 [2560, 10240], P(None, 'tp')
- W2: bfloat16 [10240, 2560], P('tp')
Outputs:
- output 1: bfloat16 [1024, 2560], P(('dp', 'tp')), parts along dimension 0
- output 2: float32 [10240, 10240], P('dp', 'tp'), parts along dimension 0
- output 3: float32 [40960, 2560], P(('dp', 'tp')), parts along dimension 0
There are 4 independent parts. A program takes and returns all parts, laid end to end along the dimension named above; an argument that names none is the same for every part.
All inputs are finite; a program needn't handle non-finite values.
Results may differ from a plain program's by a relative error of at most 0.00938058.
Values are sent between devices in bfloat16 or wider.
A program may use at most 768 MiB of HBM per device.

v0:
```python
import math
import jax
import jax.numpy as jnp
from jax import lax
from jax.sharding import PartitionSpec as P

C0 = math.sqrt(2.0 / math.pi)
C1 = 0.044715


def _gelu(u):
    t = jnp.tanh(C0 * (u + C1 * u * u * u))
    return 0.5 * u * (1.0 + t), 0.5 * (1.0 + t) + 0.5 * u * (1.0 - t * t) * C0 * (1.0 + 3.0 * C1 * u * u)


def solution(mesh):
    def body(x, dy, w1, w2):
        xg = lax.all_gather(x, 'tp', axis=0, tiled=True)
        dyg = lax.all_gather(dy, 'tp', axis=0, tiled=True)
        u = jnp.dot(xg, w1, preferred_element_type=jnp.float32).astype(jnp.bfloat16)
        g0, g1 = _gelu(u.astype(jnp.float32))
        z = g0.astype(jnp.bfloat16)
        dw2 = jnp.dot(z.T, dyg, preferred_element_type=jnp.float32)
        g = jnp.dot(dyg, w2.T, preferred_element_type=jnp.float32)
        dz = (g * g1).astype(jnp.bfloat16)
        pdx = jnp.dot(dz, w1.T, preferred_element_type=jnp.float32)
        dx = lax.psum_scatter(pdx, 'tp', scatter_dimension=0, tiled=True).astype(jnp.bfloat16)
        dw1 = jnp.dot(xg.T, dz, preferred_element_type=jnp.float32)
        return dx, dw1, dw2

    return jax.shard_map(
        body, mesh=mesh,
        in_specs=(P(('dp', 'tp'), None), P(('dp', 'tp'), None), P(None, 'tp'), P('tp', None)),
        out_specs=(P(('dp', 'tp'), None), P('dp', 'tp'), P(('dp', 'tp'), None)),
        check_vma=False)
```

profile of v0, /device:TPU:81, one launch (start us, length us, event | category | flops | bytes accessed | tf_op | source)
XLA Modules:
  0.0 103.5 jit_solution(12108020093278853647)
XLA Ops:
  7.2 0.1 all-gather.5.cloned.1.call-start
  7.2 0.7 all-gather.5.cloned.1.call-update
  8.0 0.1 all-gather.3.cloned.1.call-start
  8.0 0.7 all-gather.3.cloned.1.call-update
  8.8 0.1 reduce-scatter.2.cloned.1.call-start
  8.9 25.8 %all-gather.5.cloned.1.call-done = bf16[256,2560]{1,0:T(8,128)(2,1)} async-done(((bf16[32,2560]{1,0:T(8,128)(2,1)}), bf16[256,2560]{1,0:T(8,128)(2,1)}) %all-gather.5.cloned.1.call-update) | async-done | bytes 1310736 | tf_op jit(solution)/shard_map/all_gather | solution.py:18
  34.7 5.1 %convolution_convert_fusion = bf16[256,1280]{1,0:T(8,128)(2,1)S(1)} fusion(bf16[256,2560]{1,0:T(8,128)(2,1)} %all-gather.5.cloned.1.call-done, bf16[2560,1280]{1,0:T(8,128)(2,1)} %param.6), kind=kOutput, calls=%fused_computation.9 | convolution fusion | flops 1678049280 | bytes 8519680 | tf_op jit(solution)/shard_map/dot_general | solution.py:20
  39.8 17.1 %all-gather.3.cloned.1.call-done = bf16[256,2560]{1,0:T(8,128)(2,1)} async-done(((bf16[32,2560]{1,0:T(8,128)(2,1)}), bf16[256,2560]{1,0:T(8,128)(2,1)}) %all-gather.3.cloned.1.call-update) | async-done | bytes 1310736 | tf_op jit(solution)/shard_map/all_gather | solution.py:19
  56.9 0.0 copy-start.2
  56.9 5.7 %fusion = bf16[256,1280]{1,0:T(8,128)(2,1)S(1)} fusion(bf16[256,2560]{1,0:T(8,128)(2,1)} %all-gather.3.cloned.1.call-done, bf16[1280,2560]{1,0:T(8,128)(2,1)} %param.7, bf16[256,1280]{1,0:T(8,128)(2,1)S(1)} %convolution_convert_fusion), kind=kOutput, calls=%fused_computation.10 | convolution fusion | flops 1684275200 | bytes 9175040 | tf_op jit(solution)/shard_map/dot_general | solution.py:24
  62.6 0.0 copy-done.2
  62.6 3.4 %fusion.20 = f32[256,2560]{1,0:T(8,128)} fusion(bf16[256,1280]{1,0:T(8,128)(2,1)S(1)} %fusion, bf16[2560,1280]{1,0:T(8,128)(2,1)S(1)} %copy-done.2), kind=kOutput, calls=%fused_computation.29 | convolution fusion | flops 1677721600 | bytes 9830400 | tf_op jit(solution)/shard_map/dot_general | solution.py:26
  66.0 0.0 copy-start
  66.0 0.1 reduce-scatter.2.cloned.1.call-update
  66.1 1.3 %copy-done = bf16[256,2560]{1,0:T(8,128)(2,1)S(1)} copy-done((bf16[256,2560]{1,0:T(8,128)(2,1)S(1)}, bf16[256,2560]{1,0:T(8,128)(2,1)}, u32[]{:S(2)}) %copy-start) | copy-done | bytes 1310744
  67.3 6.9 %convolution_bitcast_fusion = f32[2560,1280]{0,1:T(8,128)} fusion(bf16[256,1280]{1,0:T(8,128)(2,1)S(1)} %fusion, bf16[256,2560]{1,0:T(8,128)(2,1)S(1)} %copy-done), kind=kOutput, calls=%fused_computation | convolution fusion | flops 1677721600 | bytes 15073280 | tf_op jit(solution)/shard_map/dot_general | solution.py:28
  74.2 0.0 copy-start.1
  74.2 14.0 %copy.7 = f32[2560,1280]{1,0:T(8,128)} copy(f32[2560,1280]{0,1:T(8,128)} %convolution_bitcast_fusion) | data formatting | bytes 26214400
  88.2 0.0 copy-done.1
  88.2 7.1 %fusion.10 = f32[1280,2560]{1,0:T(8,128)} fusion(bf16[256,2560]{1,0:T(8,128)(2,1)S(1)} %copy-done.1, bf16[256,1280]{1,0:T(8,128)(2,1)S(1)} %convolution_convert_fusion), kind=kOutput, calls=%fused_computation.20 | convolution fusion | flops 1680998400 | bytes 15073280 | tf_op jit(solution)/shard_map/dot_general | solution.py:23
  95.3 0.0 reduce-scatter.2.cloned.1.call-done
  95.3 1.7 %convert_element_type.18 = bf16[32,2560]{1,0:T(8,128)(2,1)} convert(f32[32,2560]{1,0:T(8,128)} %reduce-scatter.2.cloned.1.call-done) | non-fusion elementwise | flops 81920 | bytes 491520 | tf_op jit(solution)/shard_map/convert_element_type | solution.py:27
Async XLA Ops:
  7.2 27.5 %all-gather.5.cloned.1.call-start = ((), (), s32[]{:S(2)}) async-start(), calls=%async_computation.2 | async-start | bytes 1474560 | tf_op jit(solution)/shard_map/all_gather | solution.py:18
  8.0 48.9 %all-gather.3.cloned.1.call-start = ((), (), s32[]{:S(2)}) async-start(), calls=%async_computation.1 | async-start | bytes 1474560 | tf_op jit(solution)/shard_map/all_gather | solution.py:19
  8.8 86.5 %reduce-scatter.2.cloned.1.call-start = ((), (), s32[]{:S(2)}) async-start(), calls=%async_computation.3 | async-start | bytes 2949120 | tf_op jit(solution)/shard_map/reduce_scatter | solution.py:27
  56.9 5.7 %copy-start.2 = (bf16[2560,1280]{1,0:T(8,128)(2,1)S(1)}, bf16[2560,1280]{1,0:T(8,128)(2,1)}, u32[]{:S(2)}) copy-start(bf16[2560,1280]{1,0:T(8,128)(2,1)} %param.6) | copy-start | bytes 19660804
  66.0 1.3 %copy-start = (bf16[256,2560]{1,0:T(8,128)(2,1)S(1)}, bf16[256,2560]{1,0:T(8,128)(2,1)}, u32[]{:S(2)}) copy-start(bf16[256,2560]{1,0:T(8,128)(2,1)} %all-gather.5.cloned.1.call-done) | copy-start | bytes 3932164
  74.2 14.0 %copy-start.1 = (bf16[256,2560]{1,0:T(8,128)(2,1)S(1)}, bf16[256,2560]{1,0:T(8,128)(2,1)}, u32[]{:S(2)}) copy-start(bf16[256,2560]{1,0:T(8,128)(2,1)} %all-gather.3.cloned.1.call-done) | copy-start | bytes 3932164
Sparse Core Ops, SparseCore 0:
  9.6 25.0 all-gather.4
  36.3 20.5 all-gather.2
  66.2 28.4 reduce-scatter.1
where the time goes:
time: 105 us; the launch traced here: 104 us
  waiting for transfers between devices  44.4 us (42%)
  matrix products  28.2 us (27%)
  local copies, waits for them, and re-layouts  15.3 us (15%)
  between operations  13.8 us (13%)
  other arithmetic  1.66 us (2%)
    all_gather x1, waiting for transfers between devices, body(): xg = lax.all_gather(x, 'tp', axis=0, tiled=True)  25.8 us
    all_gather x1, waiting for transfers between devices, body(): dyg = lax.all_gather(dy, 'tp', axis=0, tiled=True)  17.1 us
    unnamed x7, local copies, waits for them, and re-layouts  15.3 us
    dot_general x1, matrix products, body(): dw2 = jnp.dot(z.T, dyg, preferred_element_type=jnp.float32)  7.12 us
    dot_general x1, matrix products, body(): dw1 = jnp.dot(xg.T, dz, preferred_element_type=jnp.float32)  6.85 us
    dot_general x1, matrix products, body(): g = jnp.dot(dyg, w2.T, preferred_element_type=jnp.float32)  5.69 us
    dot_general x1, matrix products, body(): u = jnp.dot(xg, w1, preferred_element_type=jnp.float32).astype(jnp.bfloat16)  5.12 us
    dot_general x1, matrix products, body(): pdx = jnp.dot(dz, w1.T, preferred_element_type=jnp.float32)  3.4 us
  transfers between devices with their start and end apart: 3, of which 2 were waited for; matrix products, arithmetic and copies ran while one was open for 32% of the time, Pallas kernels for 0%

commit v1 on v0

v1 whole, which is shorter than its diff:
```python
import functools
import math
import jax
import jax.numpy as jnp
from jax import lax
from jax.experimental import pallas as pl
from jax.experimental.pallas import tpu as pltpu
from jax.sharding import PartitionSpec as P

C0 = math.sqrt(2.0 / math.pi)
C1 = 0.044715
MESH = pl.DeviceIdType.MESH
F32, BF16 = jnp.float32, jnp.bfloat16


def _gelu(u):
    t = jnp.tanh(C0 * (u + C1 * u * u * u))
    return 0.5 * u * (1.0 + t), 0.5 * (1.0 + t) + 0.5 * u * (1.0 - t * t) * C0 * (1.0 + 3.0 * C1 * u * u)


def _nt(a, b):
    return lax.dot_general(a, b, (((1,), (1,)), ((), ())), preferred_element_type=F32)


def _tn(a, b):
    return lax.dot_general(a, b, (((0,), (0,)), ((), ())), preferred_element_type=F32)


def _chunks(width, sizes):
    out, at = [], 0
    for s in sizes:
        out.append(slice(at, at + s))
        at += s
    assert at == width
    return out


def _forward_kernel(n, rows, chunks, pchunks,
                    x_ref, dy_ref, w1_ref, w2_ref,
                    xg, dyg, z_ref, dz_ref, own_ref, plus_ref, minus_ref, oppa_ref, oppb_ref,
                    w1_s, w2_s, u_s, g_s, keep_s, psend, precv,
                    lsem, ssem, rsem, pss, prs):
    half = n // 2
    me = lax.axis_index('tp')
    chip, core = me // 2, me % 2
    right = ((chip + 1) % half) * 2 + core
    left = ((chip + half - 1) % half) * 2 + core
    mate = chip * 2 + (1 - core)
    h = rows // 2

    def blk(s, d, lo=0, size=rows):
        return pl.ds((s * half + d) * rows + lo, size)

    loc = [pltpu.make_async_copy(x_ref, xg.at[blk(0, 0)], lsem.at[0]),
           pltpu.make_async_copy(dy_ref, dyg.at[blk(0, 0)], lsem.at[1]),
           pltpu.make_async_copy(w1_ref, w1_s, lsem.at[2]),
           pltpu.make_async_copy(w2_ref, w2_s, lsem.at[3])]
    for c in loc:
        c.start()

    barrier = pltpu.get_barrier_semaphore()
    for peer in (mate, left, right):
        pl.semaphore_signal(barrier, inc=1, device_id={'tp': peer}, device_id_type=MESH)
    pl.semaphore_wait(barrier, 3)

    def copies(buf, a, j):
        cols = chunks[j]

        def cp(kind, src, dst, dev):
            return pltpu.make_async_remote_copy(
                src_ref=buf.at[src, cols], dst_ref=buf.at[dst, cols],
                send_sem=ssem.at[a, j, kind], recv_sem=rsem.at[a, j, kind],
                device_id={'tp': dev}, device_id_type=MESH)

        return dict(
            np=cp(0, blk(0, 0), blk(0, 3), right),
            nm=cp(1, blk(0, 0), blk(0, 1), left),
            p0=cp(2, blk(0, 0), blk(1, 0), mate),
            fp=cp(3, blk(0, 3, 0, h), blk(0, 2, 0, h), right),
            fm=cp(4, blk(0, 1, h, h), blk(0, 2, h, h), left),
            p3=cp(5, blk(0, 3), blk(1, 3), mate),
            p1=cp(6, blk(0, 1), blk(1, 1), mate),
            p2a=cp(7, blk(0, 2, 0, h), blk(1, 2, 0, h), mate),
            p2b=cp(8, blk(0, 2, h, h), blk(1, 2, h, h), mate))

    nj = len(chunks)
    cx = [copies(xg, 0, j) for j in range(nj)]
    cy = [copies(dyg, 1, j) for j in range(nj)]

    def first(c):
        c['np'].start()
        c['nm'].start()
        c['p0'].start()

    def second(c):
        c['np'].wait_recv()
        c['fp'].start()
        c['p3'].start()
        c['nm'].wait_recv()
        c['fm'].start()
        c['p1'].start()

    def third(c):
        c['fp'].wait_recv()
        c['p2a'].start()
        c['fm'].wait_recv()
        c['p2b'].start()

    def last(c):
        for k in ('p0', 'p3', 'p1', 'p2a', 'p2b'):
            c[k].wait_recv()

    loc[0].wait()
    for c in cx:
        first(c)
    loc[1].wait()
    for c in cy:
        first(c)
    for c in cx:
        second(c)
    for c in cy:
        second(c)
    loc[2].wait()
    for j, c in enumerate(cx):
        third(c)
        last(c)
        part = jnp.dot(xg[:, chunks[j]], w1_s[chunks[j], :], preferred_element_type=F32)
        if j == 0:
            u_s[...] = part
        else:
            u_s[...] += part
    for c in cy[:-1]:
        third(c)

    @pl.loop(0, u_s.shape[0] // 16)
    def _(i):
        r = pl.ds(pl.multiple_of(i * 16, 16), 16)
        u = u_s[r, :].astype(BF16).astype(F32)
        g0, g1 = _gelu(u)
        z_ref[r, :] = g0.astype(BF16)
        u_s[r, :] = g1

    loc[3].wait()
    for j, c in enumerate(cy):
        if j == nj - 1:
            third(c)
        last(c)
        part = _nt(dyg[:, chunks[j]], w2_s[:, chunks[j]])
        if j == 0:
            g_s[...] = part
        else:
            g_s[...] += part

    @pl.loop(0, u_s.shape[0] // 16)
    def _(i):
        r = pl.ds(pl.multiple_of(i * 16, 16), 16)
        dz_ref[r, :] = (g_s[r, :] * u_s[r, :]).astype(BF16)

    m = half * rows
    pc = []
    for j, cols in enumerate(pchunks):
        part = _nt(dz_ref[...], w1_s[cols, :])
        psend[:, cols] = part[m:].astype(BF16)
        c = pltpu.make_async_remote_copy(
            src_ref=psend.at[:, cols], dst_ref=precv.at[:, cols], send_sem=pss.at[j], recv_sem=prs.at[j],
            device_id={'tp': mate}, device_id_type=MESH)
        c.start()
        pc.append(c)
        keep_s[:, cols] = part[:m]
    for j, cols in enumerate(pchunks):
        pc[j].wait_recv()

        def red(d, lo=0, size=rows):
            r = slice(d * rows + lo, d * rows + lo + size)
            return keep_s[r, cols] + precv[r, cols].astype(F32)

        oppa_ref[:, cols] = red(2, 0, h).astype(BF16)
        oppb_ref[:, cols] = red(2, h, h).astype(BF16)
        plus_ref[:, cols] = red(1).astype(BF16)
        minus_ref[:, cols] = red(3).astype(BF16)
        own_ref[:, cols] = red(0)
    for c in cx + cy:
        for k in c.values():
            k.wait_send()
    for c in pc:
        c.wait_send()


def _forward(x, dy, w1, w2, n):
    rows, hid = x.shape
    ff = w1.shape[1]
    t = rows * n
    chunks = _chunks(hid, (768, 768, 512, 512))
    pchunks = _chunks(hid, (512,) * 5)
    vm = pl.BlockSpec(memory_space=pltpu.VMEM)
    hbm = pl.BlockSpec(memory_space=pltpu.MemorySpace.HBM)
    sd = jax.ShapeDtypeStruct
    dma = pltpu.SemaphoreType.DMA

    return pl.pallas_call(
        functools.partial(_forward_kernel, n, rows, chunks, pchunks),
        out_shape=(sd((t, hid), BF16), sd((t, hid), BF16), sd((t, ff), BF16), sd((t, ff), BF16),
                   sd((rows, hid), F32), sd((rows, hid), BF16), sd((rows, hid), BF16),
                   sd((rows // 2, hid), BF16), sd((rows // 2, hid), BF16)),
        in_specs=[hbm] * 4,
        out_specs=(vm,) * 9,
        scratch_shapes=[
            pltpu.VMEM((hid, ff), BF16), pltpu.VMEM((ff, hid), BF16),
            pltpu.VMEM((t, ff), F32), pltpu.VMEM((t, ff), F32),
            pltpu.VMEM((t // 2, hid), F32), pltpu.VMEM((t // 2, hid), BF16), pltpu.VMEM((t // 2, hid), BF16),
            dma((4,)), dma((2, len(chunks), 9)), dma((2, len(chunks), 9)),
            dma((len(pchunks),)), dma((len(pchunks),))],
        compiler_params=pltpu.CompilerParams(
            collective_id=0, has_side_effects=True, vmem_limit_bytes=36 << 20),
        name='gather_dz',
    )(*[pltpu.with_memory_space_constraint(v, pltpu.MemorySpace.HBM) for v in (x, dy, w1, w2)])


def _wgrad(a, b, bm, name):
    t, m = a.shape
    w = b.shape[1]

    def kernel(a_ref, b_ref, o_ref, buf, sem):
        copies = []
        for i in range(m // bm):
            r = slice(i * bm, (i + 1) * bm)
            buf[r, :] = _tn(a_ref[:, r], b_ref[...])
            copies.append(pltpu.make_async_copy(buf.at[r], o_ref.at[r], sem.at[i]))
            copies[-1].start()
        for c in copies:
            c.wait()

    vm = pl.BlockSpec(memory_space=pltpu.VMEM)
    return pl.pallas_call(
        kernel, out_shape=jax.ShapeDtypeStruct((m, w), F32), in_specs=[vm] * 2,
        out_specs=pl.BlockSpec(memory_space=pltpu.MemorySpace.HBM), name=name,
        scratch_shapes=[pltpu.VMEM((m, w), F32), pltpu.SemaphoreType.DMA((m // bm,))],
        compiler_params=pltpu.CompilerParams(vmem_limit_bytes=24 << 20),
        cost_estimate=pl.CostEstimate(flops=8 * t * m * w, bytes_accessed=4 * m * w, transcendentals=0))(a, b)


def solution(mesh):
    n = mesh.shape['tp']
    half = n // 2

    def body(x, dy, w1, w2):
        h = x.shape[0] // 2
        ahead = [(2 * k + c, 2 * ((k + 1) % half) + c) for k in range(half) for c in range(2)]
        back = [(b, a) for a, b in ahead]
        xg, dyg, z, dz, own, plus, minus, oppa, oppb = _forward(x, dy, w1, w2, n)
        ra = lax.ppermute(oppa, 'tp', ahead)
        rb = lax.ppermute(oppb, 'tp', back)
        dw2 = _wgrad(z, dyg, 256, 'dw2')
        plus = jnp.concatenate([(plus[:h].astype(F32) + ra.astype(F32)).astype(BF16), plus[h:]])
        minus = jnp.concatenate([minus[:h], (minus[h:].astype(F32) + rb.astype(F32)).astype(BF16)])
        qa = lax.ppermute(plus, 'tp', ahead)
        qb = lax.ppermute(minus, 'tp', back)
        dw1 = _wgrad(xg, dz, 256, 'dw1')
        dx = (own + qa.astype(F32) + qb.astype(F32)).astype(BF16)
        return dx, dw1, dw2

    return jax.shard_map(
        body, mesh=mesh,
        in_specs=(P(('dp', 'tp'), None), P(('dp', 'tp'), None), P(None, 'tp'), P('tp', None)),
        out_specs=(P(('dp', 'tp'), None), P('dp', 'tp'), P(('dp', 'tp'), None)),
        check_vma=False)
```

time: 105 us -> 48.8 us (0.46)
  waiting for transfers between devices: 44.4 us -> 0.01 us
  Pallas kernels: 0 us -> 42.4 us
  matrix products: 28.2 us -> 0 us
  local copies, waits for them, and re-layouts: 15.3 us -> 0.01 us
  between operations: 13.8 us -> 0.72 us
  starting transfers between devices: 0.18 us -> 4.4 us
    all_gather x2 -> x0, waiting for transfers between devices: 42.9 us -> none  [the longest x1 25.8 us: body(): xg = lax.all_gather(x, 'tp', axis=0, tiled=True)]
    pallas_call x0 -> x3, Pallas kernels: none -> 42.4 us  [the longest x1 31.8 us: _forward(): pl.pallas_call(functools.partial(_forward_kernel, n, rows, chunks, pchunk...]
    dot_general x5 -> x0, matrix products: 28.2 us -> none  [the longest x1 7.12 us: body(): dw2 = jnp.dot(z.T, dyg, preferred_element_type=jnp.float32)]
    unnamed x7 -> x0, local copies, waits for them, and re-layouts: 15.3 us -> none
    ppermute x0 -> x4, starting transfers between devices: none -> 4.4 us  [the longest x1 1.76 us: body(): rb = lax.ppermute(oppb, 'tp', back)]
    unnamed x3 -> x0, waiting for transfers between devices: 1.51 us -> none
  transfers between devices with their start and end apart: 3 -> 4, of which waited for: 2 -> 0; matrix products, arithmetic and copies ran while one was open for 32% -> 0% of each run, Pallas kernels for 0% -> 22%
where the time goes in v1:
time: 48.8 us; the launch traced here: 48.3 us
  Pallas kernels  42.4 us (87%)
  starting transfers between devices  4.4 us (9%)
  other arithmetic  0.79 us (2%)
  between operations  0.72 us (1%)
    pallas_call x1, Pallas kernels, _forward(): pl.pallas_call(functools.partial(_forward_kernel, n, rows, chunks, pchunk...  31.8 us
    pallas_call x2, Pallas kernels, _wgrad(): pl.pallas_call(kernel, out_shape=jax.ShapeDtypeStruct((m, w), F32), in_sp...  10.6 us
    ppermute x1, starting transfers between devices, body(): rb = lax.ppermute(oppb, 'tp', back)  1.76 us
    ppermute x1, starting transfers between devices, body(): ra = lax.ppermute(oppa, 'tp', ahead)  1 us
  transfers between devices with their start and end apart: 4, of which 0 were waited for; matrix products, arithmetic and copies ran while one was open for 0% of the time, Pallas kernels for 22%

profile of v1, /device:TPU:81, one launch (start us, length us, event | category | flops | bytes accessed | tf_op | source)
XLA Modules:
  0.0 48.3 jit_solution(14383817638555101109)
XLA Ops:
  0.6 31.8 %gather_dz.1 = (bf16[256,2560]{1,0:T(8,128)(2,1)S(1)}, bf16[256,2560]{1,0:T(8,128)(2,1)S(1)}, bf16[256,1280]{1,0:T(8,128)(2,1)S(1)}, bf16[256,1280]{1,0:T(8,128)...) custom-call(bf16[32,2560]{1,0:T(8,128)(2,1)} %x_ref.1, ...), custom_call_target="tpu_custom_call" | custom-call | tf_op jit(solution)/shard_map/gather_dz/pallas_call | solution.py:200
  32.4 1.0 %collective-permute-start = (bf16[16,2560]{1,0:T(8,128)(2,1)S(1)}, bf16[16,2560]{1,0:T(8,128)(2,1)S(1)}, u32[]{:S(2)}, u32[]{:S(2)}) collective-permute-start(bf16[16,2560]{1,0:T(8,128)(2,1)S(1)} %get-tuple-element.14), channel_id=1, source_target_pairs={{0,2},{1,3},{2,4},{3,5},{4,6},{5,7},{6,0},{7,1},{8,10},{9,11},{10,... | collective-permute-start | bytes 245768 | tf_op jit(solution)/shard_map/ppermute | solution.py:251
  33.4 1.8 %collective-permute-start.2 = (bf16[16,2560]{1,0:T(8,128)(2,1)S(1)}, bf16[16,2560]{1,0:T(8,128)(2,1)S(1)}, u32[]{:S(2)}, u32[]{:S(2)}) collective-permute-start(bf16[16,2560]{1,0:T(8,128)(2,1)S(1)} %get-tuple-element.16), channel_id=1, source_target_pairs={{2,0},{3,1},{4,2},{5,3},{6,4},{7,5},{0,6},{1,7},{10,8},{11,9},{12,... | collective-permute-start | bytes 245768 | tf_op jit(solution)/shard_map/ppermute | solution.py:252
  35.2 5.2 %dw1.1 = f32[2560,1280]{1,0:T(8,128)} custom-call(bf16[256,2560]{1,0:T(8,128)(2,1)S(1)} %get-tuple-element.17.a_ref, bf16[256,1280]{1,0:T(8,128)(2,1)S(1)} %get-tuple-element.18.b_ref), custom_call_target="tpu_custom_call" | custom-call | flops 6710886400 | bytes 13107200 | tf_op jit(solution)/shard_map/dw1/pallas_call | solution.py:234
  40.5 0.0 collective-permute-done.2
  40.5 1.0 %collective-permute-start.3 = (bf16[32,2560]{1,0:T(8,128)(2,1)S(1)}, bf16[32,2560]{1,0:T(8,128)(2,1)S(1)}, u32[]{:S(2)}, u32[]{:S(2)}) collective-permute-start(bf16[32,2560]{1,0:T(8,128)(2,1)S(1)} %pad_maximum_fusion.1), channel_id=1, source_target_pairs={{2,0},{3,1},{4,2},{5,3},{6,4},{7,5},{0,6},{1,7},{10,8},{11,9},{12,... | collective-permute-start | bytes 491528 | tf_op jit(solution)/shard_map/ppermute | solution.py:257
  41.5 0.0 collective-permute-done
  41.5 0.7 %collective-permute-start.1 = (bf16[32,2560]{1,0:T(8,128)(2,1)S(1)}, bf16[32,2560]{1,0:T(8,128)(2,1)S(1)}, u32[]{:S(2)}, u32[]{:S(2)}) collective-permute-start(bf16[32,2560]{1,0:T(8,128)(2,1)S(1)} %pad_maximum_fusion), channel_id=1, source_target_pairs={{0,2},{1,3},{2,4},{3,5},{4,6},{5,7},{6,0},{7,1},{8,10},{9,11},{10,... | collective-permute-start | bytes 491528 | tf_op jit(solution)/shard_map/ppermute | solution.py:256
  42.2 5.4 %dw2.1 = f32[1280,2560]{1,0:T(8,128)} custom-call(bf16[256,1280]{1,0:T(8,128)(2,1)S(1)} %get-tuple-element.19.a_ref, bf16[256,2560]{1,0:T(8,128)(2,1)S(1)} %get-tuple-element.20.b_ref), custom_call_target="tpu_custom_call" | custom-call | flops 6710886400 | bytes 13107200 | tf_op jit(solution)/shard_map/dw2/pallas_call | solution.py:234
  47.6 0.0 collective-permute-done.3
  47.6 0.0 collective-permute-done.1
  47.6 0.7 %add_convert_fusion = bf16[32,2560]{1,0:T(8,128)(2,1)} fusion(bf16[32,2560]{1,0:T(8,128)(2,1)S(1)} %collective-permute-done.3, f32[32,2560]{1,0:T(8,128)S(1)} %get-tuple-element.12, bf16[32,2560]{1,0:T(8,128)(2,1)S(1)} %collective-permute-done.1), kind=kLoop, calls=%fused_computation | loop fusion | flops 409600 | bytes 819200 | tf_op jit(solution)/shard_map/convert_element_type | solution.py:259
  (6 shorter events, 0.1 us)
Async XLA Ops:
  32.4 9.1 %collective-permute-start = (bf16[16,2560]{1,0:T(8,128)(2,1)S(1)}, bf16[16,2560]{1,0:T(8,128)(2,1)S(1)}, u32[]{:S(2)}, u32[]{:S(2)}) collective-permute-start(bf16[16,2560]{1,0:T(8,128)(2,1)S(1)} %get-tuple-element.14), channel_id=1, source_target_pairs={{0,2},{1,3},{2,4},{3,5},{4,6},{5,7},{6,0},{7,1},{8,10},{9,11},{10,... | collective-permute-start | bytes 245768 | tf_op jit(solution)/shard_map/ppermute | solution.py:251
  33.4 7.0 %collective-permute-start.2 = (bf16[16,2560]{1,0:T(8,128)(2,1)S(1)}, bf16[16,2560]{1,0:T(8,128)(2,1)S(1)}, u32[]{:S(2)}, u32[]{:S(2)}) collective-permute-start(bf16[16,2560]{1,0:T(8,128)(2,1)S(1)} %get-tuple-element.16), channel_id=1, source_target_pairs={{2,0},{3,1},{4,2},{5,3},{6,4},{7,5},{0,6},{1,7},{10,8},{11,9},{12,... | collective-permute-start | bytes 245768 | tf_op jit(solution)/shard_map/ppermute | solution.py:252
  40.5 7.1 %collective-permute-start.3 = (bf16[32,2560]{1,0:T(8,128)(2,1)S(1)}, bf16[32,2560]{1,0:T(8,128)(2,1)S(1)}, u32[]{:S(2)}, u32[]{:S(2)}) collective-permute-start(bf16[32,2560]{1,0:T(8,128)(2,1)S(1)} %pad_maximum_fusion.1), channel_id=1, source_target_pairs={{2,0},{3,1},{4,2},{5,3},{6,4},{7,5},{0,6},{1,7},{10,8},{11,9},{12,... | collective-permute-start | bytes 491528 | tf_op jit(solution)/shard_map/ppermute | solution.py:257
  41.5 6.1 %collective-permute-start.1 = (bf16[32,2560]{1,0:T(8,128)(2,1)S(1)}, bf16[32,2560]{1,0:T(8,128)(2,1)S(1)}, u32[]{:S(2)}, u32[]{:S(2)}) collective-permute-start(bf16[32,2560]{1,0:T(8,128)(2,1)S(1)} %pad_maximum_fusion), channel_id=1, source_target_pairs={{0,2},{1,3},{2,4},{3,5},{4,6},{5,7},{6,0},{7,1},{8,10},{9,11},{10,... | collective-permute-start | bytes 491528 | tf_op jit(solution)/shard_map/ppermute | solution.py:256

commit v2 on v0

v2 whole, which is shorter than its diff:
```python
import functools
import math
import jax
import jax.numpy as jnp
from jax import lax
from jax.experimental import pallas as pl
from jax.experimental.pallas import tpu as pltpu
from jax.sharding import PartitionSpec as P

C0 = math.sqrt(2.0 / math.pi)
C1 = 0.044715
MESH = pl.DeviceIdType.MESH
F32, BF16 = jnp.float32, jnp.bfloat16
XCH = (1280, 1280)
YCH = (1280, 1280)
YF = ((1280,), (768, 512))
PCH = (768, 768, 768, 256)
ORDER = ((0, 0), (0, 1), (0, 3), (1, 0), (1, 1), (1, 3), (0, 2), (1, 2))


def _gelu(u):
    t = jnp.tanh(C0 * (u + C1 * u * u * u))
    return 0.5 * u * (1.0 + t), 0.5 * (1.0 + t) + 0.5 * u * (1.0 - t * t) * C0 * (1.0 + 3.0 * C1 * u * u)


def _nt(a, b):
    return lax.dot_general(a, b, (((1,), (1,)), ((), ())), preferred_element_type=F32)


def _tn(a, b):
    return lax.dot_general(a, b, (((0,), (0,)), ((), ())), preferred_element_type=F32)


def _cols(sizes, at=0):
    out = []
    for s in sizes:
        out.append(slice(at, at + s))
        at += s
    return out


def _forward_kernel(n, rows,
                    x_ref, dy_ref, w1_ref, w2_ref,
                    xg, dyg, z_ref, dz_ref, own_ref, plus_ref, minus_ref, opp_ref,
                    w1_s, w2_s, u_s, g_s, keep_s, psend, precv,
                    lsem, ssem, rsem, pss, prs):
    half = n // 2
    me = lax.axis_index('tp')
    chip, core = me // 2, me % 2
    right = ((chip + 1) % half) * 2 + core
    left = ((chip + half - 1) % half) * 2 + core
    mate = chip * 2 + (1 - core)
    h = rows // 2
    near = (n - 2) * rows

    def blk(s, d, lo=0, size=rows):
        at = ORDER.index((s, d)) * rows + lo
        return slice(at, at + size)

    loc = [pltpu.make_async_copy(x_ref, xg.at[blk(0, 0)], lsem.at[0]),
           pltpu.make_async_copy(dy_ref, dyg.at[blk(0, 0)], lsem.at[1]),
           pltpu.make_async_copy(w1_ref, w1_s, lsem.at[2]),
           pltpu.make_async_copy(w2_ref, w2_s, lsem.at[3])]
    loc[0].start()
    loc[1].start()

    barrier = pltpu.get_barrier_semaphore()
    for peer in (mate, left, right):
        pl.semaphore_signal(barrier, inc=1, device_id={'tp': peer}, device_id_type=MESH)
    pl.semaphore_wait(barrier, 3)

    used = [0]
    started = []

    def remote(buf, src, dst, cols, dev):
        i = used[0]
        used[0] += 1
        c = pltpu.make_async_remote_copy(
            src_ref=buf.at[src, cols], dst_ref=buf.at[dst, cols], send_sem=ssem.at[i], recv_sem=rsem.at[i],
            device_id={'tp': dev}, device_id_type=MESH)
        started.append(c)
        return c

    def first(buf, sizes):
        out = []
        for cols in _cols(sizes):
            a = remote(buf, blk(0, 0), blk(0, 3), cols, right)
            b = remote(buf, blk(0, 0), blk(0, 1), cols, left)
            a.start()
            b.start()
            out.append((a, b))
        own = remote(buf, blk(0, 0), blk(1, 0), slice(None), mate)
        own.start()
        return out, own

    def second(buf, pair, cols, parts):
        fa, fb = [], []
        pair[0].wait_recv()
        for q in parts:
            fa.append(remote(buf, blk(0, 3, 0, h), blk(0, 2, 0, h), q, right))
            fa[-1].start()
        ra = remote(buf, blk(0, 3), blk(1, 3), cols, mate)
        ra.start()
        pair[1].wait_recv()
        for q in parts:
            fb.append(remote(buf, blk(0, 1, h, h), blk(0, 2, h, h), q, left))
            fb[-1].start()
        rb = remote(buf, blk(0, 1), blk(1, 1), cols, mate)
        rb.start()
        return list(zip(fa, fb)), (ra, rb)

    def third(buf, pair, cols):
        pair[0].wait_recv()
        pair[1].wait_recv()
        c = remote(buf, blk(0, 2), blk(1, 2), cols, mate)
        c.start()
        return c

    def wait_all(*cs):
        for c in cs:
            c.wait_recv()

    xc, yc = _cols(XCH), _cols(YCH)
    yf = [_cols(p, c.start) for p, c in zip(YF, yc)]
    loc[0].wait()
    nx, px = first(xg, XCH)
    loc[1].wait()
    ny, py = first(dyg, YCH)
    loc[2].start()
    loc[3].start()
    fx, rx = zip(*[second(xg, p, c, (c,)) for p, c in zip(nx, xc)])
    loc[2].wait()
    wait_all(px, *rx[0], *rx[1])
    u_s[:near, :] = jnp.dot(xg[:near, :], w1_s[...], preferred_element_type=F32)

    def act(lo, hi):
        @pl.loop(lo // 16, hi // 16)
        def _(i):
            r = pl.ds(pl.multiple_of(i * 16, 16), 16)
            u = u_s[r, :].astype(BF16).astype(F32)
            g0, g1 = _gelu(u)
            z_ref[r, :] = g0.astype(BF16)
            u_s[r, :] = g1

    fy, ry = [], []
    f, r = second(dyg, ny[0], yc[0], yf[0])
    fy += f
    ry += r
    act(0, near)
    f, r = second(dyg, ny[1], yc[1], yf[1])
    fy += f
    ry += r
    loc[3].wait()

    ox = []
    for j, c in enumerate(xc):
        ox.append(third(xg, fx[j][0], c))
    yq = [q for part in yf for q in part]
    oy = []
    for j, c in enumerate(xc):
        ox[j].wait_recv()
        part = jnp.dot(xg[near:, c], w1_s[c, :], preferred_element_type=F32)
        if j == 0:
            u_s[near:, :] = part
        else:
            u_s[near:, :] += part
        oy.append(third(dyg, fy[j], yq[j]))
    act(near, n * rows)
    wait_all(py, *ry)
    for j, q in enumerate(yq):
        if j == 1:
            for i in range(len(oy), len(yq)):
                oy.append(third(dyg, fy[i], yq[i]))
        oy[j].wait_recv()
        part = _nt(dyg[:, q], w2_s[:, q])
        if j == 0:
            g_s[...] = part
        else:
            g_s[...] += part

    @pl.loop(0, n * rows // 16)
    def _(i):
        r = pl.ds(pl.multiple_of(i * 16, 16), 16)
        dz_ref[r, :] = (g_s[r, :] * u_s[r, :]).astype(BF16)

    pcols = _cols(PCH)
    pc = []
    m = 3 * rows
    for j, cols in enumerate(pcols):
        part = _nt(dz_ref[...], w1_s[cols, :])
        psend[:m, cols] = part[m:2 * m].astype(BF16)
        psend[m:, cols] = part[2 * m + rows:].astype(BF16)
        c = pltpu.make_async_remote_copy(
            src_ref=psend.at[:, cols], dst_ref=precv.at[:, cols], send_sem=pss.at[j], recv_sem=prs.at[j],
            device_id={'tp': mate}, device_id_type=MESH)
        c.start()
        pc.append(c)
        keep_s[:m, cols] = part[:m]
        keep_s[m:, cols] = part[2 * m:2 * m + rows]
    for c in started:
        c.wait_send()
    for j, cols in enumerate(pcols):
        pc[j].wait_recv()
        tot = [keep_s[d * rows:(d + 1) * rows, cols] + precv[d * rows:(d + 1) * rows, cols].astype(F32)
               for d in range(half)]
        own_ref[:, cols] = tot[0]
        plus_ref[:, cols] = tot[1].astype(BF16)
        minus_ref[:, cols] = tot[2].astype(BF16)
        opp_ref[:, cols] = tot[3].astype(BF16)
    for c in pc:
        c.wait_send()


def _hbm(*arrays):
    return [pltpu.with_memory_space_constraint(v, pltpu.MemorySpace.HBM) for v in arrays]


def _forward(x, dy, w1, w2, n):
    rows, hid = x.shape
    ff = w1.shape[1]
    t = rows * n
    vm = pl.BlockSpec(memory_space=pltpu.VMEM)
    hbm = pl.BlockSpec(memory_space=pltpu.MemorySpace.HBM)
    sd = jax.ShapeDtypeStruct
    dma = pltpu.SemaphoreType.DMA
    ncopies = 64
    return pl.pallas_call(
        functools.partial(_forward_kernel, n, rows),
        out_shape=(sd((t, hid), BF16), sd((t, hid), BF16), sd((t, ff), BF16), sd((t, ff), BF16),
                   sd((rows, hid), F32), sd((rows, hid), BF16), sd((rows, hid), BF16), sd((rows, hid), BF16)),
        in_specs=[hbm] * 4,
        out_specs=(vm,) * 8,
        scratch_shapes=[
            pltpu.VMEM((hid, ff), BF16), pltpu.VMEM((ff, hid), BF16),
            pltpu.VMEM((t, ff), F32), pltpu.VMEM((t, ff), F32),
            pltpu.VMEM((t // 2, hid), F32), pltpu.VMEM((t // 2, hid), BF16), pltpu.VMEM((t // 2, hid), BF16),
            dma((4,)), dma((ncopies,)), dma((ncopies,)), dma((len(PCH),)), dma((len(PCH),))],
        compiler_params=pltpu.CompilerParams(
            collective_id=0, has_side_effects=True, vmem_limit_bytes=36 << 20),
        name='gather_dz',
    )(*_hbm(x, dy, w1, w2))


def _wgrads(pairs, bm):
    def kernel(*refs):
        k = len(pairs)
        ins, outs, bufs, sem = refs[:2 * k], refs[2 * k:3 * k], refs[3 * k:4 * k], refs[4 * k]
        copies = []
        for p in range(k):
            a_ref, b_ref, o_ref, buf = ins[2 * p], ins[2 * p + 1], outs[p], bufs[p]
            for i in range(o_ref.shape[0] // bm):
                r = slice(i * bm, (i + 1) * bm)
                buf[r, :] = _tn(a_ref[:, r], b_ref[...])
                copies.append(pltpu.make_async_copy(buf.at[r], o_ref.at[r], sem.at[len(copies)]))
                copies[-1].start()
        for c in copies:
            c.wait()

    vm = pl.BlockSpec(memory_space=pltpu.VMEM)
    shapes = [(a.shape[1], b.shape[1]) for a, b in pairs]
    nsem = sum(s[0] // bm for s in shapes)
    t = pairs[0][0].shape[0]
    size = sum(s[0] * s[1] for s in shapes)
    return pl.pallas_call(
        kernel, out_shape=[jax.ShapeDtypeStruct(s, F32) for s in shapes], in_specs=[vm] * (2 * len(pairs)),
        out_specs=[pl.BlockSpec(memory_space=pltpu.MemorySpace.HBM)] * len(pairs), name='wgrads',
        scratch_shapes=[pltpu.VMEM(s, F32) for s in shapes] + [pltpu.SemaphoreType.DMA((nsem,))],
        compiler_params=pltpu.CompilerParams(vmem_limit_bytes=36 << 20),
        cost_estimate=pl.CostEstimate(flops=8 * t * size, bytes_accessed=4 * size, transcendentals=0),
    )(*[v for p in pairs for v in p])


def solution(mesh):
    n = mesh.shape['tp']
    half = n // 2

    def hop(v, d):
        return lax.ppermute(v, 'tp', [(2 * k + c, 2 * ((k + d) % half) + c) for k in range(half) for c in range(2)])

    def body(x, dy, w1, w2):
        xg, dyg, z, dz, own, plus, minus, opp = _forward(x, dy, w1, w2, n)
        parts = [hop(opp, 2), hop(plus, 1), hop(minus, half - 1)]
        dw2, dw1 = _wgrads([(z, dyg), (xg, dz)], 256)
        dx = own
        for p in parts:
            dx = dx + p.astype(F32)
        return dx.astype(BF16), dw1, dw2

    return jax.shard_map(
        body, mesh=mesh,
        in_specs=(P(('dp', 'tp'), None), P(('dp', 'tp'), None), P(None, 'tp'), P('tp', None)),
        out_specs=(P(('dp', 'tp'), None), P('dp', 'tp'), P(('dp', 'tp'), None)),
        check_vma=False)
```

time: 105 us -> 41.3 us (0.39); the launches traced: 104 us -> 41.2 us
  waiting for transfers between devices: 44.4 us -> 0.01 us
  Pallas kernels: 0 us -> 35.7 us
  matrix products: 28.2 us -> 0 us
  local copies, waits for them, and re-layouts: 15.3 us -> 0 us
  between operations: 13.8 us -> 0.67 us
  starting transfers between devices: 0.18 us -> 4.08 us
    all_gather x2 -> x0, waiting for transfers between devices: 42.9 us -> none  [the longest x1 25.8 us: body(): xg = lax.all_gather(x, 'tp', axis=0, tiled=True)]
    pallas_call x0 -> x2, Pallas kernels: none -> 35.7 us  [the longest x1 26.4 us: _forward(): pl.pallas_call(functools.partial(_forward_kernel, n, rows), out_shape=(sd...]
    dot_general x5 -> x0, matrix products: 28.2 us -> none  [the longest x1 7.12 us: body(): dw2 = jnp.dot(z.T, dyg, preferred_element_type=jnp.float32)]
    unnamed x7 -> x0, local copies, waits for them, and re-layouts: 15.3 us -> none
    ppermute x0 -> x3, starting transfers between devices: none -> 4.08 us  [hop(): lax.ppermute(v, 'tp', [(2 * k + c, 2 * ((k + d) % half) + c) for k in ran...]
    unnamed x3 -> x0, waiting for transfers between devices: 1.51 us -> none
  transfers between devices with their start and end apart: 3 -> 3, of which waited for: 2 -> 0; matrix products, arithmetic and copies ran while one was open for 32% -> 0% of each run, Pallas kernels for 0% -> 23%
where the time goes in v2:
time: 41.3 us; the launch traced here: 41.2 us
  Pallas kernels  35.7 us (86%)
  starting transfers between devices  4.08 us (10%)
  other arithmetic  0.74 us (2%)
  between operations  0.67 us (2%)
    pallas_call x1, Pallas kernels, _forward(): pl.pallas_call(functools.partial(_forward_kernel, n, rows), out_shape=(sd...  26.4 us
    pallas_call x1, Pallas kernels, _wgrads(): pl.pallas_call(kernel, out_shape=[jax.ShapeDtypeStruct(s, F32) for s in s...  9.35 us
    ppermute x3, starting transfers between devices, hop(): lax.ppermute(v, 'tp', [(2 * k + c, 2 * ((k + d) % half) + c) for k in ran...  4.08 us
  transfers between devices with their start and end apart: 3, of which 0 were waited for; matrix products, arithmetic and copies ran while one was open for 0% of the time, Pallas kernels for 23%

profile of v2, /device:TPU:81, one launch (start us, length us, event | category | flops | bytes accessed | tf_op | source)
XLA Modules:
  0.0 41.2 jit_solution(2496525348569743040)
XLA Ops:
  0.6 26.4 %gather_dz.1 = (bf16[256,2560]{1,0:T(8,128)(2,1)S(1)}, bf16[256,2560]{1,0:T(8,128)(2,1)S(1)}, bf16[256,1280]{1,0:T(8,128)(2,1)S(1)}, bf16[256,1280]{1,0:T(8,128)...) custom-call(bf16[32,2560]{1,0:T(8,128)(2,1)} %x_ref.1, ...), custom_call_target="tpu_custom_call" | custom-call | tf_op jit(solution)/shard_map/gather_dz/pallas_call | solution.py:227
  27.0 1.4 %collective-permute-start = (bf16[32,2560]{1,0:T(8,128)(2,1)S(1)}, bf16[32,2560]{1,0:T(8,128)(2,1)S(1)}, u32[]{:S(2)}, u32[]{:S(2)}) collective-permute-start(bf16[32,2560]{1,0:T(8,128)(2,1)S(1)} %get-tuple-element.14), channel_id=1, source_target_pairs={{0,4},{1,5},{2,6},{3,7},{4,0},{5,1},{6,2},{7,3},{8,12},{9,13},{10,... | collective-permute-start | bytes 491528 | tf_op jit(solution)/shard_map/ppermute | solution.py:278
  28.4 0.3 collective-permute-start.1
  28.8 2.4 %collective-permute-start.2 = (bf16[32,2560]{1,0:T(8,128)(2,1)S(1)}, bf16[32,2560]{1,0:T(8,128)(2,1)S(1)}, u32[]{:S(2)}, u32[]{:S(2)}) collective-permute-start(bf16[32,2560]{1,0:T(8,128)(2,1)S(1)} %get-tuple-element.16), channel_id=1, source_target_pairs={{0,6},{1,7},{2,0},{3,1},{4,2},{5,3},{6,4},{7,5},{8,14},{9,15},{10,... | collective-permute-start | bytes 491528 | tf_op jit(solution)/shard_map/ppermute | solution.py:278
  31.1 9.3 %wgrads.1 = (f32[1280,2560]{1,0:T(8,128)}, f32[2560,1280]{1,0:T(8,128)}) custom-call(bf16[256,1280]{1,0:T(8,128)(2,1)S(1)} %get-tuple-element.17.refs_0_, bf16[256,2560]{1,0:T(8,128)(2,1)S(1)} %get-tuple-element.18.refs_1_, bf16[256,2560]{1,0:T(8,128)(2,1)S(1)} %get-tuple-element.19.refs_2_, bf16[256,1280]{1,0:T(8,128)(2,1)S(1)} %get-tuple-element.20.refs_3_), custom_call_target="tpu_custom_call" | custom-call | flops 13421772800 | bytes 26214400 | tf_op jit(solution)/shard_map/wgrads/pallas_call | solution.py:264
  40.5 0.0 collective-permute-done
  40.5 0.0 collective-permute-done.1
  40.5 0.0 collective-permute-done.2
  40.5 0.7 %add_convert_fusion = bf16[32,2560]{1,0:T(8,128)(2,1)} fusion(bf16[32,2560]{1,0:T(8,128)(2,1)S(1)} %collective-permute-done.2, bf16[32,2560]{1,0:T(8,128)(2,1)S(1)} %collective-permute-done.1, f32[32,2560]{1,0:T(8,128)S(1)} %get-tuple-element.13, bf16[32,2560]{1,0:T(8,128)(2,1)S(1)} %collective-permute-done), kind=kLoop, calls=%fused_computation | loop fusion | flops 573440 | bytes 983040 | tf_op jit(solution)/shard_map/convert_element_type | solution.py:287
Async XLA Ops:
  27.0 13.4 %collective-permute-start = (bf16[32,2560]{1,0:T(8,128)(2,1)S(1)}, bf16[32,2560]{1,0:T(8,128)(2,1)S(1)}, u32[]{:S(2)}, u32[]{:S(2)}) collective-permute-start(bf16[32,2560]{1,0:T(8,128)(2,1)S(1)} %get-tuple-element.14), channel_id=1, source_target_pairs={{0,4},{1,5},{2,6},{3,7},{4,0},{5,1},{6,2},{7,3},{8,12},{9,13},{10,... | collective-permute-start | bytes 491528 | tf_op jit(solution)/shard_map/ppermute | solution.py:278
  28.4 12.0 %collective-permute-start.1 = (bf16[32,2560]{1,0:T(8,128)(2,1)S(1)}, bf16[32,2560]{1,0:T(8,128)(2,1)S(1)}, u32[]{:S(2)}, u32[]{:S(2)}) collective-permute-start(bf16[32,2560]{1,0:T(8,128)(2,1)S(1)} %get-tuple-element.15), channel_id=1, source_target_pairs={{0,2},{1,3},{2,4},{3,5},{4,6},{5,7},{6,0},{7,1},{8,10},{9,11},{10,... | collective-permute-start | bytes 491528 | tf_op jit(solution)/shard_map/ppermute | solution.py:278
  28.8 11.7 %collective-permute-start.2 = (bf16[32,2560]{1,0:T(8,128)(2,1)S(1)}, bf16[32,2560]{1,0:T(8,128)(2,1)S(1)}, u32[]{:S(2)}, u32[]{:S(2)}) collective-permute-start(bf16[32,2560]{1,0:T(8,128)(2,1)S(1)} %get-tuple-element.16), channel_id=1, source_target_pairs={{0,6},{1,7},{2,0},{3,1},{4,2},{5,3},{6,4},{7,5},{8,14},{9,15},{10,... | collective-permute-start | bytes 491528 | tf_op jit(solution)/shard_map/ppermute | solution.py:278

commit v3 on v2

--- a/solution.py
+++ b/solution.py
@@ -12,15 +12,17 @@
 MESH = pl.DeviceIdType.MESH
 F32, BF16 = jnp.float32, jnp.bfloat16
 XCH = (1280, 1280)
-YCH = (1280, 1280)
-YF = ((1280,), (768, 512))
-PCH = (768, 768, 768, 256)
+YCH = (1024, 1024, 512)
+PCH = (1280, 1280)
 ORDER = ((0, 0), (0, 1), (0, 3), (1, 0), (1, 1), (1, 3), (0, 2), (1, 2))
 
 
 def _gelu(u):
-    t = jnp.tanh(C0 * (u + C1 * u * u * u))
-    return 0.5 * u * (1.0 + t), 0.5 * (1.0 + t) + 0.5 * u * (1.0 - t * t) * C0 * (1.0 + 3.0 * C1 * u * u)
+    q = (3.0 * C0 * C1 * u) * u
+    t = jnp.tanh(u * (C0 + q * (1.0 / 3.0)))
+    p = 0.5 + 0.5 * t
+    z = u * p
+    return z, p + (z * (1.0 - t)) * (C0 + q)
 
 
 def _nt(a, b):
@@ -51,7 +53,7 @@
     left = ((chip + half - 1) % half) * 2 + core
     mate = chip * 2 + (1 - core)
     h = rows // 2
-    near = (n - 2) * rows
+    most = (n - 2) * rows
 
     def blk(s, d, lo=0, size=rows):
         at = ORDER.index((s, d)) * rows + lo
@@ -81,107 +83,98 @@
         started.append(c)
         return c
 
-    def first(buf, sizes):
-        out = []
-        for cols in _cols(sizes):
-            a = remote(buf, blk(0, 0), blk(0, 3), cols, right)
-            b = remote(buf, blk(0, 0), blk(0, 1), cols, left)
-            a.start()
-            b.start()
-            out.append((a, b))
-        own = remote(buf, blk(0, 0), blk(1, 0), slice(None), mate)
-        own.start()
-        return out, own
-
-    def second(buf, pair, cols, parts):
-        fa, fb = [], []
-        pair[0].wait_recv()
-        for q in parts:
-            fa.append(remote(buf, blk(0, 3, 0, h), blk(0, 2, 0, h), q, right))
-            fa[-1].start()
-        ra = remote(buf, blk(0, 3), blk(1, 3), cols, mate)
-        ra.start()
-        pair[1].wait_recv()
-        for q in parts:
-            fb.append(remote(buf, blk(0, 1, h, h), blk(0, 2, h, h), q, left))
-            fb[-1].start()
-        rb = remote(buf, blk(0, 1), blk(1, 1), cols, mate)
-        rb.start()
-        return list(zip(fa, fb)), (ra, rb)
-
-    def third(buf, pair, cols):
-        pair[0].wait_recv()
-        pair[1].wait_recv()
-        c = remote(buf, blk(0, 2), blk(1, 2), cols, mate)
+    def first(buf, cols):
+        a = remote(buf, blk(0, 0), blk(0, 3), cols, right)
+        b = remote(buf, blk(0, 0), blk(0, 1), cols, left)
+        a.start()
+        b.start()
+        return a, b
+
+    def relay(buf, src, dst, cols):
+        c = remote(buf, blk(*src), blk(*dst), cols, mate)
         c.start()
         return c
+
+    def second(buf, pair, parts, both=()):
+        out = []
+        for k, (c, s, d, lo, dev, dev2) in enumerate((
+                (pair[0], (0, 3), (0, 2), 0, right, right + 1 - 2 * core),
+                (pair[1], (0, 1), (0, 2), h, left, left + 1 - 2 * core))):
+            c.wait_recv()
+            for q in parts:
+                f = [remote(buf, blk(*s, lo, h), blk(*d, lo, h), q, dev)]
+                if q in both:
+                    f.append(remote(buf, blk(*s, lo, h), blk(1, 2, lo, h), q, dev2))
+                for v in f:
+                    v.start()
+                out.append((q, f))
+        return out
+
+    def near(buf, cols):
+        at = blk(0, 1).start, blk(1, 1).start
+        c = remote(buf, slice(at[0], at[0] + 2 * rows), slice(at[1], at[1] + 2 * rows), cols, mate)
+        c.start()
+        return c
+
+    def third(buf, fwd, cols):
+        for q, f in fwd:
+            if q == cols:
+                f[0].wait_recv()
+        return relay(buf, (0, 2), (1, 2), cols)
 
     def wait_all(*cs):
         for c in cs:
             c.wait_recv()
 
     xc, yc = _cols(XCH), _cols(YCH)
-    yf = [_cols(p, c.start) for p, c in zip(YF, yc)]
+
+    def act(r):
+        g0, g1 = _gelu(u_s[r, :].astype(BF16).astype(F32))
+        z_ref[r, :] = g0.astype(BF16)
+        u_s[r, :] = g1
+
     loc[0].wait()
-    nx, px = first(xg, XCH)
+    nx = [first(xg, c) for c in xc]
+    px = relay(xg, (0, 0), (1, 0), slice(None))
     loc[1].wait()
-    ny, py = first(dyg, YCH)
+    ny = [first(dyg, slice(yc[0].start, yc[0].stop)), first(dyg, slice(yc[1].start, yc[2].stop))]
+    py = relay(dyg, (0, 0), (1, 0), slice(None))
     loc[2].start()
     loc[3].start()
-    fx, rx = zip(*[second(xg, p, c, (c,)) for p, c in zip(nx, xc)])
+    fx, rx = [], []
+    for p, c in zip(nx, xc):
+        fx += second(xg, p, (c,))
+        rx.append(near(xg, c))
     loc[2].wait()
-    wait_all(px, *rx[0], *rx[1])
-    u_s[:near, :] = jnp.dot(xg[:near, :], w1_s[...], preferred_element_type=F32)
-
-    def act(lo, hi):
-        @pl.loop(lo // 16, hi // 16)
-        def _(i):
-            r = pl.ds(pl.multiple_of(i * 16, 16), 16)
-            u = u_s[r, :].astype(BF16).astype(F32)
-            g0, g1 = _gelu(u)
-            z_ref[r, :] = g0.astype(BF16)
-            u_s[r, :] = g1
-
-    fy, ry = [], []
-    f, r = second(dyg, ny[0], yc[0], yf[0])
-    fy += f
-    ry += r
-    act(0, near)
-    f, r = second(dyg, ny[1], yc[1], yf[1])
-    fy += f
-    ry += r
+    wait_all(px, *rx)
+    u_s[:most, :] = jnp.dot(xg[:most, :], w1_s[...], preferred_element_type=F32)
+    fy = second(dyg, ny[0], yc[:1])
+
+    @pl.loop(0, most // 16)
+    def _(i):
+        act(pl.ds(pl.multiple_of(i * 16, 16), 16))
+
+    fy += second(dyg, ny[1], yc[1:], yc[2:])
+    ry = near(dyg, slice(None))
     loc[3].wait()
-
-    ox = []
-    for j, c in enumerate(xc):
-        ox.append(third(xg, fx[j][0], c))
-    yq = [q for part in yf for q in part]
-    oy = []
-    for j, c in enumerate(xc):
-        ox[j].wait_recv()
-        part = jnp.dot(xg[near:, c], w1_s[c, :], preferred_element_type=F32)
-        if j == 0:
-            u_s[near:, :] = part
-        else:
-            u_s[near:, :] += part
-        oy.append(third(dyg, fy[j], yq[j]))
-    act(near, n * rows)
-    wait_all(py, *ry)
-    for j, q in enumerate(yq):
-        if j == 1:
-            for i in range(len(oy), len(yq)):
-                oy.append(third(dyg, fy[i], yq[i]))
-        oy[j].wait_recv()
-        part = _nt(dyg[:, q], w2_s[:, q])
-        if j == 0:
-            g_s[...] = part
-        else:
-            g_s[...] += part
-
-    @pl.loop(0, n * rows // 16)
-    def _(i):
-        r = pl.ds(pl.multiple_of(i * 16, 16), 16)
-        dz_ref[r, :] = (g_s[r, :] * u_s[r, :]).astype(BF16)
+    ox = [third(xg, fx, c) for c in xc]
+    ox[0].wait_recv()
+    u_s[most:, :] = jnp.dot(xg[most:, xc[0]], w1_s[xc[0], :], preferred_element_type=F32)
+    oy = [third(dyg, fy, yc[0])]
+    ox[1].wait_recv()
+    u_s[most:, :] += jnp.dot(xg[most:, xc[1]], w1_s[xc[1], :], preferred_element_type=F32)
+    oy.append(third(dyg, fy, yc[1]))
+    wait_all(py, ry, oy[0])
+    for i in range(most, n * rows, 16):
+        act(slice(i, i + 16))
+    g_s[...] = _nt(dyg[:, yc[0]], w2_s[:, yc[0]])
+    wait_all(oy[1])
+    g_s[...] += _nt(dyg[:, yc[1]], w2_s[:, yc[1]])
+    for q, f in fy:
+        if q == yc[2]:
+            wait_all(*f)
+    g = g_s[...] + _nt(dyg[:, yc[2]], w2_s[:, yc[2]])
+    dz_ref[...] = (g * u_s[...]).astype(BF16)
 
     pcols = _cols(PCH)
     pc = []
@@ -197,9 +190,10 @@
         pc.append(c)
         keep_s[:m, cols] = part[:m]
         keep_s[m:, cols] = part[2 * m:2 * m + rows]
-    for c in started:
-        c.wait_send()
     for j, cols in enumerate(pcols):
+        if j == len(pcols) - 1:
+            for c in started:
+                c.wait_send()
         pc[j].wait_recv()
         tot = [keep_s[d * rows:(d + 1) * rows, cols] + precv[d * rows:(d + 1) * rows, cols].astype(F32)
                for d in range(half)]

time: 41.3 us -> 40.2 us (0.973)
  Pallas kernels: 35.7 us -> 34.7 us
    pallas_call x1, Pallas kernels: 26.4 us -> 25.4 us  [_forward(): pl.pallas_call(functools.partial(_forward_kernel, n, rows), out_shape=(sd...]
where the time goes in v3:
time: 40.2 us
  Pallas kernels  34.7 us (86%)
  starting transfers between devices  4.01 us (10%)
  other arithmetic  0.74 us (2%)
  between operations  0.67 us (2%)
    pallas_call x1, Pallas kernels, _forward(): pl.pallas_call(functools.partial(_forward_kernel, n, rows), out_shape=(sd...  25.4 us
    pallas_call x1, Pallas kernels, _wgrads(): pl.pallas_call(kernel, out_shape=[jax.ShapeDtypeStruct(s, F32) for s in s...  9.35 us
    ppermute x3, starting transfers between devices, hop(): lax.ppermute(v, 'tp', [(2 * k + c, 2 * ((k + d) % half) + c) for k in ran...  4.01 us
  transfers between devices with their start and end apart: 3, of which 0 were waited for; matrix products, arithmetic and copies ran while one was open for 0% of the time, Pallas kernels for 23%

profile of v3, /device:TPU:81, one launch (start us, length us, event | category | flops | bytes accessed | tf_op | source)
XLA Modules:
  0.0 40.2 jit_solution(9962032313566170624)
XLA Ops:
  0.6 25.4 %gather_dz.1 = (bf16[256,2560]{1,0:T(8,128)(2,1)S(1)}, bf16[256,2560]{1,0:T(8,128)(2,1)S(1)}, bf16[256,1280]{1,0:T(8,128)(2,1)S(1)}, bf16[256,1280]{1,0:T(8,128)...) custom-call(bf16[32,2560]{1,0:T(8,128)(2,1)} %x_ref.1, ...), custom_call_target="tpu_custom_call" | custom-call | tf_op jit(solution)/shard_map/gather_dz/pallas_call | solution.py:221
  26.0 1.3 %collective-permute-start = (bf16[32,2560]{1,0:T(8,128)(2,1)S(1)}, bf16[32,2560]{1,0:T(8,128)(2,1)S(1)}, u32[]{:S(2)}, u32[]{:S(2)}) collective-permute-start(bf16[32,2560]{1,0:T(8,128)(2,1)S(1)} %get-tuple-element.14), channel_id=1, source_target_pairs={{0,4},{1,5},{2,6},{3,7},{4,0},{5,1},{6,2},{7,3},{8,12},{9,13},{10,... | collective-permute-start | bytes 491528 | tf_op jit(solution)/shard_map/ppermute | solution.py:272
  27.4 0.3 collective-permute-start.1
  27.7 2.4 %collective-permute-start.2 = (bf16[32,2560]{1,0:T(8,128)(2,1)S(1)}, bf16[32,2560]{1,0:T(8,128)(2,1)S(1)}, u32[]{:S(2)}, u32[]{:S(2)}) collective-permute-start(bf16[32,2560]{1,0:T(8,128)(2,1)S(1)} %get-tuple-element.16), channel_id=1, source_target_pairs={{0,6},{1,7},{2,0},{3,1},{4,2},{5,3},{6,4},{7,5},{8,14},{9,15},{10,... | collective-permute-start | bytes 491528 | tf_op jit(solution)/shard_map/ppermute | solution.py:272
  30.0 9.3 %wgrads.1 = (f32[1280,2560]{1,0:T(8,128)}, f32[2560,1280]{1,0:T(8,128)}) custom-call(bf16[256,1280]{1,0:T(8,128)(2,1)S(1)} %get-tuple-element.17.refs_0_, bf16[256,2560]{1,0:T(8,128)(2,1)S(1)} %get-tuple-element.18.refs_1_, bf16[256,2560]{1,0:T(8,128)(2,1)S(1)} %get-tuple-element.19.refs_2_, bf16[256,1280]{1,0:T(8,128)(2,1)S(1)} %get-tuple-element.20.refs_3_), custom_call_target="tpu_custom_call" | custom-call | flops 13421772800 | bytes 26214400 | tf_op jit(solution)/shard_map/wgrads/pallas_call | solution.py:258
  39.4 0.0 collective-permute-done
  39.4 0.0 collective-permute-done.1
  39.4 0.0 collective-permute-done.2
  39.4 0.7 %add_convert_fusion = bf16[32,2560]{1,0:T(8,128)(2,1)} fusion(bf16[32,2560]{1,0:T(8,128)(2,1)S(1)} %collective-permute-done.2, bf16[32,2560]{1,0:T(8,128)(2,1)S(1)} %collective-permute-done.1, f32[32,2560]{1,0:T(8,128)S(1)} %get-tuple-element.13, bf16[32,2560]{1,0:T(8,128)(2,1)S(1)} %collective-permute-done), kind=kLoop, calls=%fused_computation | loop fusion | flops 573440 | bytes 983040 | tf_op jit(solution)/shard_map/convert_element_type | solution.py:281
Async XLA Ops:
  26.0 13.4 %collective-permute-start = (bf16[32,2560]{1,0:T(8,128)(2,1)S(1)}, bf16[32,2560]{1,0:T(8,128)(2,1)S(1)}, u32[]{:S(2)}, u32[]{:S(2)}) collective-permute-start(bf16[32,2560]{1,0:T(8,128)(2,1)S(1)} %get-tuple-element.14), channel_id=1, source_target_pairs={{0,4},{1,5},{2,6},{3,7},{4,0},{5,1},{6,2},{7,3},{8,12},{9,13},{10,... | collective-permute-start | bytes 491528 | tf_op jit(solution)/shard_map/ppermute | solution.py:272
  27.4 12.0 %collective-permute-start.1 = (bf16[32,2560]{1,0:T(8,128)(2,1)S(1)}, bf16[32,2560]{1,0:T(8,128)(2,1)S(1)}, u32[]{:S(2)}, u32[]{:S(2)}) collective-permute-start(bf16[32,2560]{1,0:T(8,128)(2,1)S(1)} %get-tuple-element.15), channel_id=1, source_target_pairs={{0,2},{1,3},{2,4},{3,5},{4,6},{5,7},{6,0},{7,1},{8,10},{9,11},{10,... | collective-permute-start | bytes 491528 | tf_op jit(solution)/shard_map/ppermute | solution.py:272
  27.7 11.7 %collective-permute-start.2 = (bf16[32,2560]{1,0:T(8,128)(2,1)S(1)}, bf16[32,2560]{1,0:T(8,128)(2,1)S(1)}, u32[]{:S(2)}, u32[]{:S(2)}) collective-permute-start(bf16[32,2560]{1,0:T(8,128)(2,1)S(1)} %get-tuple-element.16), channel_id=1, source_target_pairs={{0,6},{1,7},{2,0},{3,1},{4,2},{5,3},{6,4},{7,5},{8,14},{9,15},{10,... | collective-permute-start | bytes 491528 | tf_op jit(solution)/shard_map/ppermute | solution.py:272

commit v4 on v3

--- a/solution.py
+++ b/solution.py
@@ -11,9 +11,10 @@
 C1 = 0.044715
 MESH = pl.DeviceIdType.MESH
 F32, BF16 = jnp.float32, jnp.bfloat16
-XCH = (1280, 1280)
+XCH = (1536, 1024)
 YCH = (1024, 1024, 512)
-PCH = (1280, 1280)
+PCH = (1536, 1024)
+HEAD = 256
 ORDER = ((0, 0), (0, 1), (0, 3), (1, 0), (1, 1), (1, 3), (0, 2), (1, 2))
 
 
@@ -43,7 +44,7 @@
 
 def _forward_kernel(n, rows,
                     x_ref, dy_ref, w1_ref, w2_ref,
-                    xg, dyg, z_ref, dz_ref, own_ref, plus_ref, minus_ref, opp_ref,
+                    xg, dyg, z_ref, dz_ref, own_ref, plus_ref, minus_ref, opp_ref, head_ref,
                     w1_s, w2_s, u_s, g_s, keep_s, psend, precv,
                     lsem, ssem, rsem, pss, prs):
     half = n // 2
@@ -190,6 +191,7 @@
         pc.append(c)
         keep_s[:m, cols] = part[:m]
         keep_s[m:, cols] = part[2 * m:2 * m + rows]
+    head_ref[...] = _tn(z_ref[:, :HEAD], dyg[...])
     for j, cols in enumerate(pcols):
         if j == len(pcols) - 1:
             for c in started:
@@ -221,9 +223,10 @@
     return pl.pallas_call(
         functools.partial(_forward_kernel, n, rows),
         out_shape=(sd((t, hid), BF16), sd((t, hid), BF16), sd((t, ff), BF16), sd((t, ff), BF16),
-                   sd((rows, hid), F32), sd((rows, hid), BF16), sd((rows, hid), BF16), sd((rows, hid), BF16)),
+                   sd((rows, hid), F32), sd((rows, hid), BF16), sd((rows, hid), BF16), sd((rows, hid), BF16),
+                   sd((HEAD, hid), F32)),
         in_specs=[hbm] * 4,
-        out_specs=(vm,) * 8,
+        out_specs=(vm,) * 9,
         scratch_shapes=[
             pltpu.VMEM((hid, ff), BF16), pltpu.VMEM((ff, hid), BF16),
             pltpu.VMEM((t, ff), F32), pltpu.VMEM((t, ff), F32),
@@ -235,33 +238,37 @@
     )(*_hbm(x, dy, w1, w2))
 
 
-def _wgrads(pairs, bm):
-    def kernel(*refs):
-        k = len(pairs)
+def _wgrads(head, pairs, bm):
+    k = len(pairs)
+    shapes = [(a.shape[1], b.shape[1]) for a, b in pairs]
+    skip = [head.shape[0]] + [0] * (k - 1)
+
+    def kernel(head_ref, *refs):
         ins, outs, bufs, sem = refs[:2 * k], refs[2 * k:3 * k], refs[3 * k:4 * k], refs[4 * k]
-        copies = []
+        copies = [pltpu.make_async_copy(head_ref, outs[0].at[:skip[0]], sem.at[0])]
+        copies[0].start()
         for p in range(k):
             a_ref, b_ref, o_ref, buf = ins[2 * p], ins[2 * p + 1], outs[p], bufs[p]
-            for i in range(o_ref.shape[0] // bm):
-                r = slice(i * bm, (i + 1) * bm)
-                buf[r, :] = _tn(a_ref[:, r], b_ref[...])
-                copies.append(pltpu.make_async_copy(buf.at[r], o_ref.at[r], sem.at[len(copies)]))
+            for i in range(skip[p], shapes[p][0], bm):
+                r, w = slice(i, i + bm), slice(i - skip[p], i - skip[p] + bm)
+                buf[w, :] = _tn(a_ref[:, r], b_ref[...])
+                copies.append(pltpu.make_async_copy(buf.at[w], o_ref.at[r], sem.at[len(copies)]))
                 copies[-1].start()
         for c in copies:
             c.wait()
 
     vm = pl.BlockSpec(memory_space=pltpu.VMEM)
-    shapes = [(a.shape[1], b.shape[1]) for a, b in pairs]
-    nsem = sum(s[0] // bm for s in shapes)
+    nsem = 1 + sum((s[0] - d) // bm for s, d in zip(shapes, skip))
     t = pairs[0][0].shape[0]
     size = sum(s[0] * s[1] for s in shapes)
     return pl.pallas_call(
-        kernel, out_shape=[jax.ShapeDtypeStruct(s, F32) for s in shapes], in_specs=[vm] * (2 * len(pairs)),
-        out_specs=[pl.BlockSpec(memory_space=pltpu.MemorySpace.HBM)] * len(pairs), name='wgrads',
-        scratch_shapes=[pltpu.VMEM(s, F32) for s in shapes] + [pltpu.SemaphoreType.DMA((nsem,))],
+        kernel, out_shape=[jax.ShapeDtypeStruct(s, F32) for s in shapes], in_specs=[vm] * (2 * k + 1),
+        out_specs=[pl.BlockSpec(memory_space=pltpu.MemorySpace.HBM)] * k, name='wgrads',
+        scratch_shapes=[pltpu.VMEM((s[0] - d, s[1]), F32) for s, d in zip(shapes, skip)]
+        + [pltpu.SemaphoreType.DMA((nsem,))],
         compiler_params=pltpu.CompilerParams(vmem_limit_bytes=36 << 20),
         cost_estimate=pl.CostEstimate(flops=8 * t * size, bytes_accessed=4 * size, transcendentals=0),
-    )(*[v for p in pairs for v in p])
+    )(head, *[v for p in pairs for v in p])
 
 
 def solution(mesh):
@@ -272,9 +279,9 @@
         return lax.ppermute(v, 'tp', [(2 * k + c, 2 * ((k + d) % half) + c) for k in range(half) for c in range(2)])
 
     def body(x, dy, w1, w2):
-        xg, dyg, z, dz, own, plus, minus, opp = _forward(x, dy, w1, w2, n)
+        xg, dyg, z, dz, own, plus, minus, opp, head = _forward(x, dy, w1, w2, n)
         parts = [hop(opp, 2), hop(plus, 1), hop(minus, half - 1)]
-        dw2, dw1 = _wgrads([(z, dyg), (xg, dz)], 256)
+        dw2, dw1 = _wgrads(head, [(z, dyg), (xg, dz)], 256)
         dx = own
         for p in parts:
             dx = dx + p.astype(F32)

time: 40.2 us -> 39.5 us (0.983)
  Pallas kernels: 34.7 us -> 33.9 us
    pallas_call x1, Pallas kernels: 9.35 us -> 8.84 us  [_wgrads(): pl.pallas_call(kernel, out_shape=[jax.ShapeDtypeStruct(s, F32) for s in s...]
  transfers between devices with their start and end apart: 3 -> 3, of which waited for: 0 -> 0; matrix products, arithmetic and copies ran while one was open for 0% -> 0% of each run, Pallas kernels for 23% -> 22%
where the time goes in v4:
time: 39.5 us; the launch traced here: 39.4 us
  Pallas kernels  33.9 us (86%)
  starting transfers between devices  4.07 us (10%)
  other arithmetic  0.74 us (2%)
  between operations  0.67 us (2%)
    pallas_call x1, Pallas kernels, _forward(): pl.pallas_call(functools.partial(_forward_kernel, n, rows), out_shape=(sd...  25.1 us
    pallas_call x1, Pallas kernels, _wgrads(): pl.pallas_call(kernel, out_shape=[jax.ShapeDtypeStruct(s, F32) for s in s...  8.84 us
    ppermute x3, starting transfers between devices, hop(): lax.ppermute(v, 'tp', [(2 * k + c, 2 * ((k + d) % half) + c) for k in ran...  4.07 us
  transfers between devices with their start and end apart: 3, of which 0 were waited for; matrix products, arithmetic and copies ran while one was open for 0% of the time, Pallas kernels for 22%

profile of v4, /device:TPU:81, one launch (start us, length us, event | category | flops | bytes accessed | tf_op | source)
XLA Modules:
  0.0 39.4 jit_solution(17113558514295336047)
XLA Ops:
  0.6 25.1 %gather_dz.1 = (bf16[256,2560]{1,0:T(8,128)(2,1)S(1)}, bf16[256,2560]{1,0:T(8,128)(2,1)S(1)}, bf16[256,1280]{1,0:T(8,128)(2,1)S(1)}, bf16[256,1280]{1,0:T(8,128)...) custom-call(bf16[32,2560]{1,0:T(8,128)(2,1)} %x_ref.1, ...), custom_call_target="tpu_custom_call" | custom-call | tf_op jit(solution)/shard_map/gather_dz/pallas_call | solution.py:223
  25.7 1.4 %collective-permute-start = (bf16[32,2560]{1,0:T(8,128)(2,1)S(1)}, bf16[32,2560]{1,0:T(8,128)(2,1)S(1)}, u32[]{:S(2)}, u32[]{:S(2)}) collective-permute-start(bf16[32,2560]{1,0:T(8,128)(2,1)S(1)} %get-tuple-element.15), channel_id=1, source_target_pairs={{0,4},{1,5},{2,6},{3,7},{4,0},{5,1},{6,2},{7,3},{8,12},{9,13},{10,... | collective-permute-start | bytes 491528 | tf_op jit(solution)/shard_map/ppermute | solution.py:279
  27.1 0.4 %collective-permute-start.1 = (bf16[32,2560]{1,0:T(8,128)(2,1)S(1)}, bf16[32,2560]{1,0:T(8,128)(2,1)S(1)}, u32[]{:S(2)}, u32[]{:S(2)}) collective-permute-start(bf16[32,2560]{1,0:T(8,128)(2,1)S(1)} %get-tuple-element.16), channel_id=1, source_target_pairs={{0,2},{1,3},{2,4},{3,5},{4,6},{5,7},{6,0},{7,1},{8,10},{9,11},{10,... | collective-permute-start | bytes 491528 | tf_op jit(solution)/shard_map/ppermute | solution.py:279
  27.5 2.3 %collective-permute-start.2 = (bf16[32,2560]{1,0:T(8,128)(2,1)S(1)}, bf16[32,2560]{1,0:T(8,128)(2,1)S(1)}, u32[]{:S(2)}, u32[]{:S(2)}) collective-permute-start(bf16[32,2560]{1,0:T(8,128)(2,1)S(1)} %get-tuple-element.17), channel_id=1, source_target_pairs={{0,6},{1,7},{2,0},{3,1},{4,2},{5,3},{6,4},{7,5},{8,14},{9,15},{10,... | collective-permute-start | bytes 491528 | tf_op jit(solution)/shard_map/ppermute | solution.py:279
  29.8 8.8 %wgrads.1 = (f32[1280,2560]{1,0:T(8,128)}, f32[2560,1280]{1,0:T(8,128)}) custom-call(f32[256,2560]{1,0:T(8,128)S(1)} %get-tuple-element.18.head_ref, bf16[256,1280]{1,0:T(8,128)(2,1)S(1)} %get-tuple-element.19.refs_0_, bf16[256,2560]{1,0:T(8,128)(2,1)S(1)} %get-tuple-element.20.refs_1_, bf16[256,2560]{1,0:T(8,128)(2,1)S(1)} %get-tuple-element.21.refs_2_, ...), custom_call_target="tpu_custom_call" | custom-call | flops 13421772800 | bytes 26214400 | tf_op jit(solution)/shard_map/wgrads/pallas_call | solution.py:264
  38.7 0.0 collective-permute-done
  38.7 0.0 collective-permute-done.1
  38.7 0.0 collective-permute-done.2
  38.7 0.7 %add_convert_fusion = bf16[32,2560]{1,0:T(8,128)(2,1)} fusion(bf16[32,2560]{1,0:T(8,128)(2,1)S(1)} %collective-permute-done.2, bf16[32,2560]{1,0:T(8,128)(2,1)S(1)} %collective-permute-done.1, f32[32,2560]{1,0:T(8,128)S(1)} %get-tuple-element.14, bf16[32,2560]{1,0:T(8,128)(2,1)S(1)} %collective-permute-done), kind=kLoop, calls=%fused_computation | loop fusion | flops 573440 | bytes 983040 | tf_op jit(solution)/shard_map/convert_element_type | solution.py:288
Async XLA Ops:
  25.7 12.9 %collective-permute-start = (bf16[32,2560]{1,0:T(8,128)(2,1)S(1)}, bf16[32,2560]{1,0:T(8,128)(2,1)S(1)}, u32[]{:S(2)}, u32[]{:S(2)}) collective-permute-start(bf16[32,2560]{1,0:T(8,128)(2,1)S(1)} %get-tuple-element.15), channel_id=1, source_target_pairs={{0,4},{1,5},{2,6},{3,7},{4,0},{5,1},{6,2},{7,3},{8,12},{9,13},{10,... | collective-permute-start | bytes 491528 | tf_op jit(solution)/shard_map/ppermute | solution.py:279
  27.1 11.5 %collective-permute-start.1 = (bf16[32,2560]{1,0:T(8,128)(2,1)S(1)}, bf16[32,2560]{1,0:T(8,128)(2,1)S(1)}, u32[]{:S(2)}, u32[]{:S(2)}) collective-permute-start(bf16[32,2560]{1,0:T(8,128)(2,1)S(1)} %get-tuple-element.16), channel_id=1, source_target_pairs={{0,2},{1,3},{2,4},{3,5},{4,6},{5,7},{6,0},{7,1},{8,10},{9,11},{10,... | collective-permute-start | bytes 491528 | tf_op jit(solution)/shard_map/ppermute | solution.py:279
  27.5 11.1 %collective-permute-start.2 = (bf16[32,2560]{1,0:T(8,128)(2,1)S(1)}, bf16[32,2560]{1,0:T(8,128)(2,1)S(1)}, u32[]{:S(2)}, u32[]{:S(2)}) collective-permute-start(bf16[32,2560]{1,0:T(8,128)(2,1)S(1)} %get-tuple-element.17), channel_id=1, source_target_pairs={{0,6},{1,7},{2,0},{3,1},{4,2},{5,3},{6,4},{7,5},{8,14},{9,15},{10,... | collective-permute-start | bytes 491528 | tf_op jit(solution)/shard_map/ppermute | solution.py:279

commit v5 on v4

--- a/solution.py
+++ b/solution.py
@@ -12,7 +12,7 @@
 MESH = pl.DeviceIdType.MESH
 F32, BF16 = jnp.float32, jnp.bfloat16
 XCH = (1536, 1024)
-YCH = (1024, 1024, 512)
+YCH = (1024, 768, 768)
 PCH = (1536, 1024)
 HEAD = 256
 ORDER = ((0, 0), (0, 1), (0, 3), (1, 0), (1, 1), (1, 3), (0, 2), (1, 2))
@@ -280,7 +280,7 @@
 
     def body(x, dy, w1, w2):
         xg, dyg, z, dz, own, plus, minus, opp, head = _forward(x, dy, w1, w2, n)
-        parts = [hop(opp, 2), hop(plus, 1), hop(minus, half - 1)]
+        parts = [hop(plus, 1), hop(minus, half - 1), hop(opp, 2)]
         dw2, dw1 = _wgrads(head, [(z, dyg), (xg, dz)], 256)
         dx = own
         for p in parts:

time: 39.5 us -> 38.2 us (0.967)
  starting transfers between devices: 4.07 us -> 2.76 us
    ppermute x3, starting transfers between devices: 4.07 us -> 2.76 us  [hop(): lax.ppermute(v, 'tp', [(2 * k + c, 2 * ((k + d) % half) + c) for k in ran...]
  transfers between devices with their start and end apart: 3 -> 3, of which waited for: 0 -> 0; matrix products, arithmetic and copies ran while one was open for 0% -> 0% of each run, Pallas kernels for 22% -> 23%
where the time goes in v5:
time: 38.2 us; the launch traced here: 38.1 us
  Pallas kernels  33.9 us (89%)
  starting transfers between devices  2.76 us (7%)
  other arithmetic  0.74 us (2%)
  between operations  0.68 us (2%)
    pallas_call x1, Pallas kernels, _forward(): pl.pallas_call(functools.partial(_forward_kernel, n, rows), out_shape=(sd...  25.1 us
    pallas_call x1, Pallas kernels, _wgrads(): pl.pallas_call(kernel, out_shape=[jax.ShapeDtypeStruct(s, F32) for s in s...  8.84 us
    ppermute x3, starting transfers between devices, hop(): lax.ppermute(v, 'tp', [(2 * k + c, 2 * ((k + d) % half) + c) for k in ran...  2.76 us
  transfers between devices with their start and end apart: 3, of which 0 were waited for; matrix products, arithmetic and copies ran while one was open for 0% of the time, Pallas kernels for 23%

profile of v5, /device:TPU:81, one launch (start us, length us, event | category | flops | bytes accessed | tf_op | source)
XLA Modules:
  0.0 38.1 jit_solution(115752099063940242)
XLA Ops:
  0.6 25.1 %gather_dz.1 = (bf16[256,2560]{1,0:T(8,128)(2,1)S(1)}, bf16[256,2560]{1,0:T(8,128)(2,1)S(1)}, bf16[256,1280]{1,0:T(8,128)(2,1)S(1)}, bf16[256,1280]{1,0:T(8,128)...) custom-call(bf16[32,2560]{1,0:T(8,128)(2,1)} %x_ref.1, ...), custom_call_target="tpu_custom_call" | custom-call | tf_op jit(solution)/shard_map/gather_dz/pallas_call | solution.py:223
  25.7 0.1 collective-permute-start
  25.9 2.6 %collective-permute-start.1 = (bf16[32,2560]{1,0:T(8,128)(2,1)S(1)}, bf16[32,2560]{1,0:T(8,128)(2,1)S(1)}, u32[]{:S(2)}, u32[]{:S(2)}) collective-permute-start(bf16[32,2560]{1,0:T(8,128)(2,1)S(1)} %get-tuple-element.16), channel_id=1, source_target_pairs={{0,6},{1,7},{2,0},{3,1},{4,2},{5,3},{6,4},{7,5},{8,14},{9,15},{10,... | collective-permute-start | bytes 491528 | tf_op jit(solution)/shard_map/ppermute | solution.py:279
  28.5 0.0 collective-permute-start.2
  28.5 8.8 %wgrads.1 = (f32[1280,2560]{1,0:T(8,128)}, f32[2560,1280]{1,0:T(8,128)}) custom-call(f32[256,2560]{1,0:T(8,128)S(1)} %get-tuple-element.18.head_ref, bf16[256,1280]{1,0:T(8,128)(2,1)S(1)} %get-tuple-element.19.refs_0_, bf16[256,2560]{1,0:T(8,128)(2,1)S(1)} %get-tuple-element.20.refs_1_, bf16[256,2560]{1,0:T(8,128)(2,1)S(1)} %get-tuple-element.21.refs_2_, ...), custom_call_target="tpu_custom_call" | custom-call | flops 13421772800 | bytes 26214400 | tf_op jit(solution)/shard_map/wgrads/pallas_call | solution.py:264
  37.4 0.0 collective-permute-done
  37.4 0.0 collective-permute-done.1
  37.4 0.0 collective-permute-done.2
  37.4 0.7 %add_convert_fusion = bf16[32,2560]{1,0:T(8,128)(2,1)} fusion(bf16[32,2560]{1,0:T(8,128)(2,1)S(1)} %collective-permute-done.2, bf16[32,2560]{1,0:T(8,128)(2,1)S(1)} %collective-permute-done.1, f32[32,2560]{1,0:T(8,128)S(1)} %get-tuple-element.14, bf16[32,2560]{1,0:T(8,128)(2,1)S(1)} %collective-permute-done), kind=kLoop, calls=%fused_computation | loop fusion | flops 573440 | bytes 983040 | tf_op jit(solution)/shard_map/convert_element_type | solution.py:288
Async XLA Ops:
  25.7 11.6 %collective-permute-start = (bf16[32,2560]{1,0:T(8,128)(2,1)S(1)}, bf16[32,2560]{1,0:T(8,128)(2,1)S(1)}, u32[]{:S(2)}, u32[]{:S(2)}) collective-permute-start(bf16[32,2560]{1,0:T(8,128)(2,1)S(1)} %get-tuple-element.15), channel_id=1, source_target_pairs={{0,2},{1,3},{2,4},{3,5},{4,6},{5,7},{6,0},{7,1},{8,10},{9,11},{10,... | collective-permute-start | bytes 491528 | tf_op jit(solution)/shard_map/ppermute | solution.py:279
  25.9 11.5 %collective-permute-start.1 = (bf16[32,2560]{1,0:T(8,128)(2,1)S(1)}, bf16[32,2560]{1,0:T(8,128)(2,1)S(1)}, u32[]{:S(2)}, u32[]{:S(2)}) collective-permute-start(bf16[32,2560]{1,0:T(8,128)(2,1)S(1)} %get-tuple-element.16), channel_id=1, source_target_pairs={{0,6},{1,7},{2,0},{3,1},{4,2},{5,3},{6,4},{7,5},{8,14},{9,15},{10,... | collective-permute-start | bytes 491528 | tf_op jit(solution)/shard_map/ppermute | solution.py:279
  28.5 8.9 %collective-permute-start.2 = (bf16[32,2560]{1,0:T(8,128)(2,1)S(1)}, bf16[32,2560]{1,0:T(8,128)(2,1)S(1)}, u32[]{:S(2)}, u32[]{:S(2)}) collective-permute-start(bf16[32,2560]{1,0:T(8,128)(2,1)S(1)} %get-tuple-element.17), channel_id=1, source_target_pairs={{0,4},{1,5},{2,6},{3,7},{4,0},{5,1},{6,2},{7,3},{8,12},{9,13},{10,... | collective-permute-start | bytes 491528 | tf_op jit(solution)/shard_map/ppermute | solution.py:279

commit v6 on v5

--- a/solution.py
+++ b/solution.py
@@ -155,7 +155,7 @@
     def _(i):
         act(pl.ds(pl.multiple_of(i * 16, 16), 16))
 
-    fy += second(dyg, ny[1], yc[1:], yc[2:])
+    fy += second(dyg, ny[1], yc[1:], yc[1:])
     ry = near(dyg, slice(None))
     loc[3].wait()
     ox = [third(xg, fx, c) for c in xc]
@@ -164,12 +164,13 @@
     oy = [third(dyg, fy, yc[0])]
     ox[1].wait_recv()
     u_s[most:, :] += jnp.dot(xg[most:, xc[1]], w1_s[xc[1], :], preferred_element_type=F32)
-    oy.append(third(dyg, fy, yc[1]))
     wait_all(py, ry, oy[0])
     for i in range(most, n * rows, 16):
         act(slice(i, i + 16))
     g_s[...] = _nt(dyg[:, yc[0]], w2_s[:, yc[0]])
-    wait_all(oy[1])
+    for q, f in fy:
+        if q == yc[1]:
+            wait_all(*f)
     g_s[...] += _nt(dyg[:, yc[1]], w2_s[:, yc[1]])
     for q, f in fy:
         if q == yc[2]:

time: 38.2 us -> 38 us (level)
  no operation moved by 1% of the time
where the time goes in v6:
time: 38 us; the launch traced here: 37.9 us
  Pallas kernels  33.7 us (89%)
  starting transfers between devices  2.77 us (7%)
  other arithmetic  0.74 us (2%)
  between operations  0.67 us (2%)
    pallas_call x1, Pallas kernels, _forward(): pl.pallas_call(functools.partial(_forward_kernel, n, rows), out_shape=(sd...  24.9 us
    pallas_call x1, Pallas kernels, _wgrads(): pl.pallas_call(kernel, out_shape=[jax.ShapeDtypeStruct(s, F32) for s in s...  8.84 us
    ppermute x3, starting transfers between devices, hop(): lax.ppermute(v, 'tp', [(2 * k + c, 2 * ((k + d) % half) + c) for k in ran...  2.77 us
  transfers between devices with their start and end apart: 3, of which 0 were waited for; matrix products, arithmetic and copies ran while one was open for 0% of the time, Pallas kernels for 23%

profile of v6, /device:TPU:81, one launch (start us, length us, event | category | flops | bytes accessed | tf_op | source)
XLA Modules:
  0.0 37.9 jit_solution(17295372603708403472)
XLA Ops:
  0.6 24.9 %gather_dz.1 = (bf16[256,2560]{1,0:T(8,128)(2,1)S(1)}, bf16[256,2560]{1,0:T(8,128)(2,1)S(1)}, bf16[256,1280]{1,0:T(8,128)(2,1)S(1)}, bf16[256,1280]{1,0:T(8,128)...) custom-call(bf16[32,2560]{1,0:T(8,128)(2,1)} %x_ref.1, ...), custom_call_target="tpu_custom_call" | custom-call | tf_op jit(solution)/shard_map/gather_dz/pallas_call | solution.py:224
  25.5 0.2 collective-permute-start
  25.8 2.5 %collective-permute-start.1 = (bf16[32,2560]{1,0:T(8,128)(2,1)S(1)}, bf16[32,2560]{1,0:T(8,128)(2,1)S(1)}, u32[]{:S(2)}, u32[]{:S(2)}) collective-permute-start(bf16[32,2560]{1,0:T(8,128)(2,1)S(1)} %get-tuple-element.16), channel_id=1, source_target_pairs={{0,6},{1,7},{2,0},{3,1},{4,2},{5,3},{6,4},{7,5},{8,14},{9,15},{10,... | collective-permute-start | bytes 491528 | tf_op jit(solution)/shard_map/ppermute | solution.py:280
  28.3 0.0 collective-permute-start.2
  28.3 8.8 %wgrads.1 = (f32[1280,2560]{1,0:T(8,128)}, f32[2560,1280]{1,0:T(8,128)}) custom-call(f32[256,2560]{1,0:T(8,128)S(1)} %get-tuple-element.18.head_ref, bf16[256,1280]{1,0:T(8,128)(2,1)S(1)} %get-tuple-element.19.refs_0_, bf16[256,2560]{1,0:T(8,128)(2,1)S(1)} %get-tuple-element.20.refs_1_, bf16[256,2560]{1,0:T(8,128)(2,1)S(1)} %get-tuple-element.21.refs_2_, ...), custom_call_target="tpu_custom_call" | custom-call | flops 13421772800 | bytes 26214400 | tf_op jit(solution)/shard_map/wgrads/pallas_call | solution.py:265
  37.2 0.0 collective-permute-done
  37.2 0.0 collective-permute-done.1
  37.2 0.0 collective-permute-done.2
  37.2 0.7 %add_convert_fusion = bf16[32,2560]{1,0:T(8,128)(2,1)} fusion(bf16[32,2560]{1,0:T(8,128)(2,1)S(1)} %collective-permute-done.2, bf16[32,2560]{1,0:T(8,128)(2,1)S(1)} %collective-permute-done.1, f32[32,2560]{1,0:T(8,128)S(1)} %get-tuple-element.14, bf16[32,2560]{1,0:T(8,128)(2,1)S(1)} %collective-permute-done), kind=kLoop, calls=%fused_computation | loop fusion | flops 573440 | bytes 983040 | tf_op jit(solution)/shard_map/convert_element_type | solution.py:289
Async XLA Ops:
  25.5 11.6 %collective-permute-start = (bf16[32,2560]{1,0:T(8,128)(2,1)S(1)}, bf16[32,2560]{1,0:T(8,128)(2,1)S(1)}, u32[]{:S(2)}, u32[]{:S(2)}) collective-permute-start(bf16[32,2560]{1,0:T(8,128)(2,1)S(1)} %get-tuple-element.15), channel_id=1, source_target_pairs={{0,2},{1,3},{2,4},{3,5},{4,6},{5,7},{6,0},{7,1},{8,10},{9,11},{10,... | collective-permute-start | bytes 491528 | tf_op jit(solution)/shard_map/ppermute | solution.py:280
  25.8 11.4 %collective-permute-start.1 = (bf16[32,2560]{1,0:T(8,128)(2,1)S(1)}, bf16[32,2560]{1,0:T(8,128)(2,1)S(1)}, u32[]{:S(2)}, u32[]{:S(2)}) collective-permute-start(bf16[32,2560]{1,0:T(8,128)(2,1)S(1)} %get-tuple-element.16), channel_id=1, source_target_pairs={{0,6},{1,7},{2,0},{3,1},{4,2},{5,3},{6,4},{7,5},{8,14},{9,15},{10,... | collective-permute-start | bytes 491528 | tf_op jit(solution)/shard_map/ppermute | solution.py:280
  28.3 8.9 %collective-permute-start.2 = (bf16[32,2560]{1,0:T(8,128)(2,1)S(1)}, bf16[32,2560]{1,0:T(8,128)(2,1)S(1)}, u32[]{:S(2)}, u32[]{:S(2)}) collective-permute-start(bf16[32,2560]{1,0:T(8,128)(2,1)S(1)} %get-tuple-element.17), channel_id=1, source_target_pairs={{0,4},{1,5},{2,6},{3,7},{4,0},{5,1},{6,2},{7,3},{8,12},{9,13},{10,... | collective-permute-start | bytes 491528 | tf_op jit(solution)/shard_map/ppermute | solution.py:280
